TPU v7x, 32 devices: a whole 2x2x4 slice. The times are simulated.
32 devices in a mesh: band: 4 (over z), px: 4 (over x, core), py: 2 (over y).
Axes of the slice: x: 2, y: 2, z: 4, core: 2. Of those that a mesh axis runs over, the one named last changes fastest.
Arguments:
- orbitals: bfloat16 [4, 1024, 384], P('band', ('px', 'py')), may hold values from -0.01171875 to 0.01171875
- occupations: float32 [4], P('band'), may hold values from 0.2 to 2
- stick_map: int32 [2, 1024], P(None, 'px'), may hold values from 0 to 191, as said below
- core_density: float32 [192, 192, 192], P('py', 'px'), may hold values from 0.05 to 0.5
Outputs:
- potential: float32 [192, 192, 192], P('py', 'px')
- gradient: float32 [3, 192, 192, 192], P(None, 'py', 'px')
Inputs may be any that keep to these rules, and one draw needn't show every extreme that they name: `stick_map`: columns i * 128 * 2 to (i + 1) * 128 * 2 - 1 have x index from i * 48 to (i + 1) * 48 - 1; no two columns share a grid position.
All inputs are finite; a program needn't handle non-finite values.
Results may differ from a plain program's by a relative error of at most 0.0054.
Values may be sent and summed in bfloat16 or wider, within the bound.
No kernel may reach another device: no remote copies, remote signals or barrier semaphores. Data moves between devices by JAX's collectives and lax.ppermute only.
A program may use at most 128 MiB of HBM per device.

v0:
```python
import math
import jax
import jax.numpy as jnp
from jax import lax
from jax.sharding import PartitionSpec as P

SPACING = 0.25
PBE_KAPPA = 0.804
PBE_MU = 0.2195
SLATER_COEF = 0.75 * (3.0 / math.pi) ** (1.0 / 3.0)
REDUCED_SCALE = 4.0 * (3.0 * math.pi**2) ** (2.0 / 3.0)
HIGHEST_PREC = lax.Precision.HIGHEST


def complex_table(row_index, col_index, points, direction):
    product = row_index[:, None] * col_index[None, :] % points
    angles = 2.0 * math.pi / points * product.astype(jnp.float32)
    cosine = jnp.cos(angles)
    sine_part = direction * jnp.sin(angles)
    return jnp.stack([jnp.stack([cosine, sine_part], 1), jnp.stack([-sine_part, cosine], 1)], 0)


def freq_pair(positions, points):
    signed = jnp.where(positions <= points // 2, positions, positions - points).astype(jnp.float32)
    gradient_freq = jnp.where(positions == points // 2, 0.0, signed)
    return (signed, gradient_freq)


def swap_rows(values):
    return lax.all_to_all(values, "px", split_axis=1, concat_axis=0, tiled=True)


def swap_depth(values):
    moved = lax.all_to_all(values, ("band", "py"), split_axis=1, concat_axis=0, tiled=True)
    return moved


def exchange_part(density, fields):
    cube_root = jnp.cbrt(density)
    four_thirds = density * cube_root
    grad_square = fields[1] * fields[1] + fields[2] * fields[2] + fields[3] * fields[3]
    reduced = grad_square / (REDUCED_SCALE * four_thirds * four_thirds)
    denominator = 1.0 + PBE_MU * reduced / PBE_KAPPA
    enhance = 1.0 + PBE_KAPPA - PBE_KAPPA / denominator
    enhance_slope = PBE_MU / (denominator * denominator)
    potential = fields[0] - SLATER_COEF * cube_root * (
        4.0 / 3.0 * enhance - 8.0 / 3.0 * reduced * enhance_slope
    )
    return jnp.concatenate([potential[None], fields[1:]], 0)


def transform(rho_local, pieces, depth_index, px_index):
    zshare, y_rows, points = rho_local.shape
    rows_px = lax.axis_size("px")
    rows_py = lax.axis_size("py")
    xblock = points // rows_px
    kyblock = points // pieces
    zblock = zshare * (pieces // rows_py)
    every_index = jnp.arange(points, dtype=jnp.int32)
    forward = complex_table(every_index, every_index, points, -1.0)
    x_table = forward[0].reshape(points, 2, rows_px, xblock).transpose(0, 2, 1, 3)
    section_data = jnp.einsum("zyx,xbsk->ybzsk", rho_local, x_table, precision=HIGHEST_PREC)
    section_data = swap_rows(section_data.reshape(y_rows, rows_px, zshare * 2 * xblock))
    section_data = section_data.reshape(points, zshare, 2, xblock)
    y_table = forward.reshape(2, points, 2, pieces, kyblock)
    section_data = jnp.einsum("yzrx,rysdk->zdksx", section_data, y_table, precision=HIGHEST_PREC)
    section_data = swap_depth(section_data.reshape(zshare, pieces, kyblock * 2 * xblock))
    section_data = section_data.reshape(pieces * zshare, kyblock, 2, xblock)
    source = jnp.arange(pieces * zshare, dtype=jnp.int32)
    device = source // zshare
    within = source % zshare
    z_order = device % rows_py * zblock + device // rows_py * zshare + within
    z_table = complex_table(z_order, every_index, points, -1.0)
    spectrum = jnp.einsum("zyrx,rzsk->kysx", section_data, z_table, precision=HIGHEST_PREC)
    q_depth, g_depth = freq_pair(every_index, points)
    ky_index = depth_index * kyblock + jnp.arange(kyblock, dtype=jnp.int32)
    q_col, g_col = freq_pair(ky_index, points)
    kx_index = px_index * xblock + jnp.arange(xblock, dtype=jnp.int32)
    q_row, g_row = freq_pair(kx_index, points)
    wave_unit = 2.0 * math.pi / (points * SPACING)
    squared = wave_unit**2 * (
        q_depth[:, None, None] ** 2 + q_col[None, :, None] ** 2 + q_row[None, None, :] ** 2
    )
    hartree = jnp.where(squared > 0, 4.0 * math.pi / jnp.where(squared > 0, squared, 1.0), 0.0)
    wave_z = wave_unit * g_depth[:, None, None]
    wave_y = wave_unit * g_col[None, :, None]
    wave_x = wave_unit * g_row[None, None, :]
    real_part = spectrum[:, :, 0, :]
    imag_part = spectrum[:, :, 1, :]
    first_factor = hartree - wave_x
    packed = jnp.stack(
        [
            jnp.stack([first_factor * real_part, first_factor * imag_part], 2),
            jnp.stack(
                [-wave_z * real_part - wave_y * imag_part, wave_y * real_part - wave_z * imag_part],
                2,
            ),
        ],
        0,
    )
    inverse = complex_table(every_index, every_index, points, 1.0)
    zi_table = complex_table(every_index, z_order, points, 1.0).reshape(
        2, points, 2, pieces, zshare
    )
    section_data = jnp.einsum("fkyrx,rksdz->ydfzsx", packed, zi_table, precision=HIGHEST_PREC)
    section_data = swap_depth(section_data.reshape(kyblock, pieces, 2 * zshare * 2 * xblock))
    section_data = section_data.reshape(points, 2, zshare, 2, xblock)
    yi_table = inverse.reshape(2, points, 2, rows_px, y_rows)
    section_data = jnp.einsum("kfzrx,rksby->xbfzsy", section_data, yi_table, precision=HIGHEST_PREC)
    section_data = swap_rows(section_data.reshape(xblock, rows_px, 2 * zshare * 2 * y_rows))
    section_data = section_data.reshape(points, 2, zshare, 2, y_rows)
    fields = jnp.einsum("kfzry,rksx->fszyx", section_data, inverse, precision=HIGHEST_PREC)
    fields = fields * (1.0 / float(points) ** 3)
    return fields.reshape(4, zshare, y_rows, points)


def body(orbitals, occupations, stick_map, core_density):
    bands_here, columns_here, doubled = orbitals.shape
    points = doubled // 2
    rows_px = lax.axis_size("px")
    rows_py = lax.axis_size("py")
    groups = lax.axis_size("band")
    px_index = lax.axis_index("px")
    py_index = lax.axis_index("py")
    xblock = points // rows_px
    zblock = points // rows_py
    y_rows = points // rows_px
    every_index = jnp.arange(points, dtype=jnp.int32)
    inverse = complex_table(every_index, every_index, points, 1.0)
    z_table = (
        inverse.reshape(2, points, 2, rows_py, zblock)
        .transpose(0, 1, 3, 2, 4)
        .reshape(doubled, doubled)
    )
    columns = jnp.dot(
        orbitals.astype(jnp.float32).reshape(bands_here * columns_here, doubled),
        z_table,
        precision=HIGHEST_PREC,
    )
    columns = columns.astype(jnp.bfloat16).reshape(bands_here, columns_here, doubled)
    columns = lax.all_to_all(columns, "py", split_axis=2, concat_axis=1, tiled=True)
    slot_index = stick_map[1] * xblock + (stick_map[0] - px_index * xblock)
    plane_data = (
        jnp.zeros((bands_here, points * xblock, 2 * zblock), jnp.float32)
        .at[:, slot_index]
        .set(columns.astype(jnp.float32))
    )
    plane_data = plane_data.reshape(bands_here, points, xblock, 2, zblock)
    plane_data = jnp.einsum("byxrz,rysk->bkxsz", plane_data, inverse, precision=HIGHEST_PREC)
    plane_data = plane_data.astype(jnp.bfloat16).reshape(bands_here, points, xblock * 2 * zblock)
    plane_data = lax.all_to_all(plane_data, "px", split_axis=1, concat_axis=2, tiled=True)
    plane_data = plane_data.astype(jnp.float32).reshape(bands_here, y_rows, points, 2, zblock)
    orbital_values = jnp.einsum("byxrz,rxsk->bszyk", plane_data, inverse, precision=HIGHEST_PREC)
    density = jnp.einsum(
        "b,bszyk->zyk", occupations, orbital_values * orbital_values, precision=HIGHEST_PREC
    )
    zshare = zblock // groups
    band_index = lax.axis_index("band")
    shared_rows = lax.psum_scatter(density, "band", scatter_dimension=0, tiled=True)
    core_rows = lax.dynamic_slice_in_dim(core_density, band_index * zshare, zshare, 0)
    rho_local = shared_rows + core_rows
    fields = transform(rho_local, groups * rows_py, band_index * rows_py + py_index, px_index)
    results = lax.all_gather(exchange_part(rho_local, fields), "band", axis=1, tiled=True)
    return (results[0], results[1:4])


def solution(mesh):
    return jax.shard_map(
        body,
        mesh=mesh,
        in_specs=(P("band", ("px", "py"), None), P("band"), P(None, "px"), P("py", "px", None)),
        out_specs=(P("py", "px", None), P(None, "py", "px", None)),
        check_vma=False,
    )
```

profile of v0, /device:TPU:0, one launch (start us, length us, event | category | flops | bytes accessed | tf_op | source)
XLA Modules:
  0.0 1160.9 jit_solution(13728535052132577211)
XLA Ops:
  27.8 12.3 %reshape.807 = f32[192,48,2,96]{3,2,1,0:T(2,128)} reshape(f32[9216,192]{1,0:T(8,128)} %scatter_custom_fusion) | data formatting | bytes 14155776 | tf_op jit(solution)/shard_map/reshape.2
  40.1 14.2 %copy.140 = f32[192,48,2,96]{0,3,2,1:T(8,128)} copy(f32[192,48,2,96]{3,2,1,0:T(2,128)} %reshape.807) | data formatting | bytes 14155776 | tf_op jit(solution)/shard_map/reshape.2
  54.3 18.6 %fusion.5 = bf16[1,192,48,2,96]{1,4,2,3,0:T(8,128)(2,1)} fusion(f32[192,48,2,96]{0,3,2,1:T(8,128)} %copy.140, f32[1,192,2,192]{3,1,0,2:T(8,128)S(1)} %get-tuple-element.11, f32[1,192,2,192]{3,1,0,2:T(8,128)S(1)} %get-tuple-element.10), kind=kOutput, calls=%fused_computation.8 | convolution fusion | flops 8155643904 | bytes 11206656 | tf_op jit(solution)/shard_map/byxrz,rysk->bkxsz/dot_general | solution.py:149
  72.8 11.6 copy.141
  84.4 24.4 %reshape.857 = bf16[1,192,9216]{2,0,1:T(2,128)(2,1)} reshape(bf16[1,192,48,2,96]{4,3,2,1,0:T(2,128)(2,1)} %copy.141) | data formatting | bytes 7077888 | tf_op jit(solution)/shard_map/reshape | solution.py:150
  108.8 78.5 %reduce.4 = bf16[192,9216]{1,0:T(8,128)(2,1)} reduce(bf16[192,1,9216]{2,1,0:T(2,128)(2,1)} %bitcast.221, bf16[]{:T(256)} %broadcast.1309), dimensions={1}, to_apply=%bitcast.207.reduce_sub_computation | reduce | bytes 7077890
  198.3 40.5 %all-to-all-done.1 = bf16[4,2,221184]{2,1,0:T(2,128)(2,1)} async-done(((bf16[4,2,221184]{2,1,0:T(2,128)(2,1)}), bf16[4,2,221184]{2,1,0:T(2,128)(2,1)}, u32[]{:S(2)}, u32[]{:S(2)}) %all-to-all-start.1) | async-done | bytes 3538976 | tf_op jit(solution)/shard_map/all_to_all | solution.py:151
  254.0 14.9 %reshape.809 = bf16[48,192,2,96]{3,2,1,0:T(2,128)(2,1)} reshape(bf16[1,48,4,9216]{3,2,1,0:T(4,128)(2,1)} %copy.143) | data formatting | bytes 7077888 | tf_op jit(solution)/shard_map/reshape.5
  268.9 10.5 fusion.2
  289.7 84.4 %reduce-scatter.2.cloned.1.call-done = f32[24,48,192]{2,1,0:T(8,128)} async-done(((f32[96,48,192]{2,1,0:T(8,128)}), f32[24,48,192]{2,1,0:T(8,128)}) %reduce-scatter.2.cloned.1.call-update) | async-done | bytes 884752 | tf_op jit(solution)/shard_map/reduce_scatter | solution.py:159
  380.9 7.5 copy.147
  388.4 9.3 reshape.811
  402.4 21.2 %all-to-all-done.2 = f32[48,4,2304]{2,0,1:T(8,128)S(1)} async-done(((f32[48,4,2304]{2,0,1:T(8,128)}), f32[48,4,2304]{2,0,1:T(8,128)S(1)}, u32[]{:S(2)}, u32[]{:S(2)}) %all-to-all-start.2) | async-done | bytes 1769504 | tf_op jit(solution)/shard_map/all_to_all | solution.py:30
  423.6 8.6 reshape.812
  432.2 10.4 fusion.27
  448.4 9.7 reshape.858
  466.9 37.3 %all-to-all-done.3 = f32[24,8,2304]{2,0,1:T(8,128)S(1)} async-done(((f32[24,8,2304]{2,0,1:T(8,128)}), f32[24,8,2304]{2,0,1:T(8,128)S(1)}, u32[]{:S(2)}, u32[]{:S(2)}) %all-to-all-start.3) | async-done | bytes 1769504 | tf_op jit(solution)/shard_map/all_to_all | solution.py:34
  504.1 8.6 reshape.814
  525.6 15.9 %fusion.22 = f32[24,8,2,24,2,48]{5,3,0,2,1,4:T(8,128)S(1)} fusion(f32[1,192,24,2,48]{1,4,2,3,0:T(8,128)S(1)} %maximum_bitcast_fusion.5, f32[1,192,24,2,48]{1,4,2,3,0:T(8,128)S(1)} %maximum_bitcast_fusion.4, f32[1,192,1,8,24]{1,4,0,3,2:T(8,128)S(1)} %copy-done.4, f32[1,192,1,8,24]{1,4,0,3,2:T(8,128)S(1)} %copy-done.3, ...), kind=kOutput, calls=%fused_computation.28 | convolution fusion | flops 4078190592 | bytes 7520256 | tf_op jit(solution)/shard_map/fkyrx,rksdz->ydfzsx/dot_general | solution.py:105
  541.5 8.0 copy.189
  549.5 16.6 %reshape.859 = f32[24,8,4608]{2,0,1:T(8,128)} reshape(f32[24,8,2,24,2,48]{5,4,3,2,0,1:T(2,128)} %copy.189) | data formatting | bytes 7077888 | tf_op jit(solution)/shard_map/reshape | solution.py:106
  571.5 77.6 %all-to-all-done.4 = f32[24,8,4608]{2,0,1:T(8,128)} async-done(((f32[24,8,4608]{2,0,1:T(8,128)}), f32[24,8,4608]{2,0,1:T(8,128)}, u32[]{:S(2)}, u32[]{:S(2)}) %all-to-all-start.4) | async-done | bytes 3538976 | tf_op jit(solution)/shard_map/all_to_all | solution.py:34
  649.2 17.3 %reshape.816 = f32[192,2,24,2,48]{4,3,2,1,0:T(2,128)} reshape(f32[8,24,1,4608]{3,1,0,2:T(8,128)} %bitcast.63) | data formatting | bytes 7077888 | tf_op jit(solution)/shard_map/reshape | solution.py:107
  666.5 24.9 %fusion.19 = f32[48,4,2,24,2,48]{0,5,3,2,1,4:T(8,128)} fusion(f32[192,2,24,2,48,1,1]{4,3,2,1,0,6,5:T(2,128)} %bitcast.218, f32[1,192,1,4,48]{1,4,0,3,2:T(8,128)S(1)} %get-tuple-element.20, f32[1,192,1,4,48]{1,4,0,3,2:T(8,128)S(1)} %get-tuple-element.19, f32[1,192,1,4,48]{1,4,0,3,2:T(8,128)S(1)} %get-tuple-element.18), kind=kOutput, calls=%fused_computation.27 | convolution fusion | flops 4077305856 | bytes 7520256 | tf_op jit(solution)/shard_map/kfzrx,rksby->xbfzsy/dot_general | solution.py:109
  691.4 13.7 %copy.157 = f32[48,4,2,24,2,48]{5,4,3,2,0,1:T(2,128)} copy(f32[48,4,2,24,2,48]{0,5,3,2,1,4:T(8,128)} %fusion.19) | data formatting | bytes 7077888 | tf_op jit(solution)/shard_map/kfzrx,rksby->xbfzsy/transpose | solution.py:109
  705.1 16.6 %reshape.817 = f32[48,4,4608]{2,0,1:T(8,128)} reshape(f32[48,4,2,24,2,48]{5,4,3,2,0,1:T(2,128)} %copy.157) | data formatting | bytes 7077888 | tf_op jit(solution)/shard_map/reshape | solution.py:110
  721.7 46.9 %all_to_all.84 = f32[48,4,4608]{2,0,1:T(8,128)} all-to-all(f32[48,4,4608]{2,0,1:T(8,128)} %reshape.817), channel_id=1, replica_groups=mesh['band'=4,'px'=4,'py'=2] {'px'}, dimensions={1} | all-to-all | bytes 7077888 | tf_op jit(solution)/shard_map/all_to_all | solution.py:30
  768.6 17.1 %reshape.818 = f32[192,2,24,2,48]{4,3,2,1,0:T(2,128)} reshape(f32[4,48,1,4608]{3,1,0,2:T(8,128)} %bitcast.224) | data formatting | bytes 7077888 | tf_op jit(solution)/shard_map/reshape | solution.py:111
  785.7 13.2 %copy.158 = f32[192,2,24,2,48]{0,4,3,2,1:T(8,128)} copy(f32[192,2,24,2,48]{4,3,2,1,0:T(2,128)} %reshape.818) | data formatting | bytes 7077888 | tf_op jit(solution)/shard_map/reshape | solution.py:111
  798.9 10.3 fusion.9
  816.6 320.4 %all-gather.2.cloned.1.call-done = f32[4,96,48,192]{3,2,1,0:T(8,128)} async-done(((f32[4,24,48,192]{3,2,1,0:T(8,128)}), f32[4,96,48,192]{3,2,1,0:T(8,128)}) %all-gather.2.cloned.1.call-update) | async-done | bytes 14155792 | tf_op jit(solution)/shard_map/all_gather | solution.py:163
  1141.8 11.8 %slice.55 = f32[3,96,48,192]{3,2,1,0:T(8,128)} slice(f32[4,96,48,192]{3,2,1,0:T(8,128)} %all-gather.2.cloned.1.call-done), slice={[1:4], [0:96], [0:48], [0:192]} | slice | bytes 21233664 | tf_op jit(solution)/shard_map/slice | solution.py:164
  (74 shorter events, 112.7 us)
Async XLA Ops:
  7.2 2.2 copy-start
  8.1 10.4 copy-start.5
  12.6 8.6 all-to-all-start
  192.9 45.9 %all-to-all-start.1 = ((bf16[4,2,221184]{2,1,0:T(2,128)(2,1)}), bf16[4,2,221184]{2,1,0:T(2,128)(2,1)}, u32[]{:S(2)}, u32[]{:S(2)}) async-start(bf16[4,2,221184]{2,1,0:T(2,128)(2,1)} %reshape.864), calls=%async_computation.1 | async-start | bytes 7077888 | tf_op jit(solution)/shard_map/all_to_all | solution.py:151
  197.6 176.5 %reduce-scatter.2.cloned.1.call-start = ((), (), s32[]{:S(2)}) async-start(), calls=%async_computation.7 | async-start | bytes 5898240 | tf_op jit(solution)/shard_map/reduce_scatter | solution.py:159
  397.7 25.9 %all-to-all-start.2 = ((f32[48,4,2304]{2,0,1:T(8,128)}), f32[48,4,2304]{2,0,1:T(8,128)S(1)}, u32[]{:S(2)}, u32[]{:S(2)}) async-start(f32[48,4,2304]{2,0,1:T(8,128)} %reshape.811), calls=%async_computation.3 | async-start | bytes 3538944 | tf_op jit(solution)/shard_map/all_to_all | solution.py:30
  458.1 46.0 %all-to-all-start.3 = ((f32[24,8,2304]{2,0,1:T(8,128)}), f32[24,8,2304]{2,0,1:T(8,128)S(1)}, u32[]{:S(2)}, u32[]{:S(2)}) async-start(f32[24,8,2304]{2,0,1:T(8,128)} %reshape.858), calls=%async_computation.4 | async-start | bytes 3538944 | tf_op jit(solution)/shard_map/all_to_all | solution.py:34
  524.6 0.9 copy-start.3
  524.6 1.0 copy-start.4
  566.1 83.1 %all-to-all-start.4 = ((f32[24,8,4608]{2,0,1:T(8,128)}), f32[24,8,4608]{2,0,1:T(8,128)}, u32[]{:S(2)}, u32[]{:S(2)}) async-start(f32[24,8,4608]{2,0,1:T(8,128)} %reshape.859), calls=%async_computation.5 | async-start | bytes 7077888 | tf_op jit(solution)/shard_map/all_to_all | solution.py:34
  570.6 566.4 %all-gather.2.cloned.1.call-start = ((), (), s32[]{:S(2)}) async-start(), calls=%async_computation.8 | async-start | bytes 23592960 | tf_op jit(solution)/shard_map/all_gather | solution.py:163
  809.6 1.3 copy-start.2
  1141.8 11.8 %copy-start.1 = (bf16[1,128,384]{2,1,0:T(8,128)(2,1)S(1)}, bf16[1,128,384]{2,1,0:T(8,128)(2,1)}, u32[]{:S(2)}) copy-start(bf16[1,128,384]{2,1,0:T(8,128)(2,1)} %param.4) | copy-start | bytes 294916
Sparse Core Ops, SparseCore 0:
  288.9 85.1 reduce-scatter.1
  816.7 320.2 all-gather.1
where the time goes:
time: 1170 us; the launch traced here: 1160 us
  waiting for transfers between devices  584 us (50%)
  local copies, waits for them, and re-layouts  291 us (25%)
  matrix products  103 us (9%)
  other arithmetic  98.1 us (8%)
  blocking collectives  46.9 us (4%)
  starting transfers between devices  22.4 us (2%)
  between operations  15.5 us (1%)
    all_gather x1, waiting for transfers between devices, body(): lax.all_gather(exchange_part(rho_local, fields), 'band', axis=1, tiled=True)  320 us
    all_to_all x2, waiting for transfers between devices, swap_depth(): lax.all_to_all(values, ('band', 'py'), split_axis=1, concat_axis=0, tiled...  115 us
    reduce_scatter x1, waiting for transfers between devices, body(): lax.psum_scatter(density, 'band', scatter_dimension=0, tiled=True)  84.4 us
    unnamed x2, other arithmetic  79.7 us
    all_to_all x1, blocking collectives, swap_rows(): return lax.all_to_all(values, 'px', split_axis=1, concat_axis=0, tiled=True)  46.9 us
    another operation x3, local copies, waits for them, and re-layouts  41.4 us
    all_to_all x1, waiting for transfers between devices, body(): lax.all_to_all(plane_data, 'px', split_axis=1, concat_axis=2, tiled=True)  40.5 us
    reshape x2, local copies, waits for them, and re-layouts, transform(): section_data = section_data.reshape(points, 2, zshare, 2, y_rows)  30.3 us
  transfers between devices with their start and end apart: 7, of which 7 were waited for; matrix products, arithmetic and copies ran while one was open for 1% of the time, Pallas kernels for 0%

commit v1 on v0

--- a/solution.py
+++ b/solution.py
@@ -31,7 +31,15 @@
 
 
 def swap_depth(values):
-    moved = lax.all_to_all(values, ("band", "py"), split_axis=1, concat_axis=0, tiled=True)
+    moved = jnp.concatenate(
+        lax.all_to_all(
+            jnp.stack(jnp.split(values, lax.axis_size(("band", "py")), axis=1)),
+            ("band", "py"),
+            0,
+            0,
+        ),
+        axis=0,
+    )
     return moved
 
 

time: 1170 us -> 1220 us (1.043)
  local copies, waits for them, and re-layouts: 291 us -> 324 us
  other arithmetic: 98.1 us -> 116 us
    another operation x3 -> x8, local copies, waits for them, and re-layouts: 41.4 us -> 78.1 us
    reshape x3 -> x0, local copies, waits for them, and re-layouts: 31.6 us -> none  [the longest x1 17.3 us: transform(): section_data = section_data.reshape(points, 2, zshare, 2, xblock)]
    unnamed x18 -> x32, local copies, waits for them, and re-layouts: 19.5 us -> 47.4 us
    all_to_all x0 -> x2, other arithmetic: none -> 17.5 us  [swap_depth(): lax.all_to_all(jnp.stack(jnp.split(values, lax.axis_size(('band', 'py')),...]
    transpose x0 -> x2, local copies, waits for them, and re-layouts: none -> 14.8 us  [the longest x1 8.97 us: transform(): jnp.einsum('fkyrx,rksdz->ydfzsx', packed, zi_table, precision=HIGHEST_PREC)]
    reshape x2 -> x1, local copies, waits for them, and re-layouts: 24.6 us -> 16.6 us  [transform(): section_data.reshape(kyblock, pieces, 2 * zshare * 2 * xblock)]
where the time goes in v1:
time: 1220 us; the launch traced here: 1210 us
  waiting for transfers between devices  584 us (48%)
  local copies, waits for them, and re-layouts  324 us (27%)
  other arithmetic  116 us (10%)
  matrix products  103 us (8%)
  blocking collectives  46.8 us (4%)
  starting transfers between devices  22.6 us (2%)
  between operations  15.3 us (1%)
    all_gather x1, waiting for transfers between devices, body(): lax.all_gather(exchange_part(rho_local, fields), 'band', axis=1, tiled=True)  320 us
    all_to_all x2, waiting for transfers between devices, swap_depth(): lax.all_to_all(jnp.stack(jnp.split(values, lax.axis_size(('band', 'py')),...  115 us
    reduce_scatter x1, waiting for transfers between devices, body(): lax.psum_scatter(density, 'band', scatter_dimension=0, tiled=True)  84.4 us
    unnamed x2, other arithmetic  79.6 us
    unnamed x32, local copies, waits for them, and re-layouts  47.4 us
    all_to_all x1, blocking collectives, swap_rows(): return lax.all_to_all(values, 'px', split_axis=1, concat_axis=0, tiled=True)  46.8 us
    another operation x3, local copies, waits for them, and re-layouts  41.4 us
    all_to_all x1, waiting for transfers between devices, body(): lax.all_to_all(plane_data, 'px', split_axis=1, concat_axis=2, tiled=True)  40.5 us
  transfers between devices with their start and end apart: 7, of which 7 were waited for; matrix products, arithmetic and copies ran while one was open for 1% of the time, Pallas kernels for 0%

profile of v1, /device:TPU:0, one launch (start us, length us, event | category | flops | bytes accessed | tf_op | source)
XLA Modules:
  0.0 1211.5 jit_solution(542931258034393094)
XLA Ops:
  28.2 12.3 %reshape.799 = f32[192,48,2,96]{3,2,1,0:T(2,128)} reshape(f32[9216,192]{1,0:T(8,128)} %scatter_custom_fusion) | data formatting | bytes 14155776 | tf_op jit(solution)/shard_map/reshape.2
  40.4 14.2 %copy.144 = f32[192,48,2,96]{0,3,2,1:T(8,128)} copy(f32[192,48,2,96]{3,2,1,0:T(2,128)} %reshape.799) | data formatting | bytes 14155776 | tf_op jit(solution)/shard_map/reshape.2
  54.6 18.6 %fusion.5 = bf16[1,192,48,2,96]{1,4,2,3,0:T(8,128)(2,1)} fusion(f32[192,48,2,96]{0,3,2,1:T(8,128)} %copy.144, f32[1,192,2,192]{3,1,0,2:T(8,128)S(1)} %get-tuple-element.11, f32[1,192,2,192]{3,1,0,2:T(8,128)S(1)} %get-tuple-element.10), kind=kOutput, calls=%fused_computation.8 | convolution fusion | flops 8155643904 | bytes 11206656 | tf_op jit(solution)/shard_map/byxrz,rysk->bkxsz/dot_general | solution.py:157
  73.2 11.6 copy.145
  84.8 24.4 %reshape.847 = bf16[1,192,9216]{2,0,1:T(2,128)(2,1)} reshape(bf16[1,192,48,2,96]{4,3,2,1,0:T(2,128)(2,1)} %copy.145) | data formatting | bytes 7077888 | tf_op jit(solution)/shard_map/reshape | solution.py:158
  109.2 78.3 %reduce.6 = bf16[192,9216]{1,0:T(8,128)(2,1)} reduce(bf16[192,1,9216]{2,1,0:T(2,128)(2,1)} %bitcast.267, bf16[]{:T(256)} %broadcast.1311), dimensions={1}, to_apply=%bitcast.253.reduce_sub_computation | reduce | bytes 7077890
  198.5 40.5 %all-to-all-done.1 = bf16[4,2,221184]{2,1,0:T(2,128)(2,1)} async-done(((bf16[4,2,221184]{2,1,0:T(2,128)(2,1)}), bf16[4,2,221184]{2,1,0:T(2,128)(2,1)}, u32[]{:S(2)}, u32[]{:S(2)}) %all-to-all-start.1) | async-done | bytes 3538976 | tf_op jit(solution)/shard_map/all_to_all | solution.py:159
  254.2 14.9 %reshape.801 = bf16[48,192,2,96]{3,2,1,0:T(2,128)(2,1)} reshape(bf16[1,48,4,9216]{3,2,1,0:T(4,128)(2,1)} %copy.147) | data formatting | bytes 7077888 | tf_op jit(solution)/shard_map/reshape.5
  269.2 10.6 fusion.2
  290.0 84.4 %reduce-scatter.2.cloned.1.call-done = f32[24,48,192]{2,1,0:T(8,128)} async-done(((f32[96,48,192]{2,1,0:T(8,128)}), f32[24,48,192]{2,1,0:T(8,128)}) %reduce-scatter.2.cloned.1.call-update) | async-done | bytes 884752 | tf_op jit(solution)/shard_map/reduce_scatter | solution.py:167
  388.6 9.3 reshape.803
  402.9 21.2 %all-to-all-done.2 = f32[48,4,2304]{2,0,1:T(8,128)S(1)} async-done(((f32[48,4,2304]{2,0,1:T(8,128)}), f32[48,4,2304]{2,0,1:T(8,128)S(1)}, u32[]{:S(2)}, u32[]{:S(2)}) %all-to-all-start.2) | async-done | bytes 1769504 | tf_op jit(solution)/shard_map/all_to_all | solution.py:30
  424.1 8.6 reshape.804
  432.6 10.4 fusion.27
  448.9 8.6 reshape.805
  473.2 37.2 %all-to-all-done.3 = f32[8,24,1,2304]{3,2,1,0:T(1,128)S(1)} async-done(((f32[8,24,1,2304]{3,2,1,0:T(1,128)}), f32[8,24,1,2304]{3,2,1,0:T(1,128)S(1)}, u32[]{:S(2)}, u32[]{:S(2)}) %all-to-all-start.3) | async-done | bytes 1769504 | tf_op jit(solution)/shard_map/all_to_all | solution.py:35
  516.3 9.6 reshape_reshape.6
  539.1 15.7 %fusion.22 = f32[24,8,2,24,2,48]{5,3,0,2,1,4:T(8,128)S(1)} fusion(f32[1,192,24,2,48]{1,4,2,3,0:T(8,128)S(1)} %maximum_bitcast_fusion.5, f32[1,192,24,2,48]{1,4,2,3,0:T(8,128)S(1)} %maximum_bitcast_fusion.4, f32[1,192,1,8,24]{1,4,0,3,2:T(8,128)S(1)} %copy-done.4, f32[1,192,1,8,24]{1,4,0,3,2:T(8,128)S(1)} %copy-done.3, ...), kind=kOutput, calls=%fused_computation.28 | convolution fusion | flops 4078190592 | bytes 7520256 | tf_op jit(solution)/shard_map/fkyrx,rksdz->ydfzsx/dot_general | solution.py:113
  554.8 9.0 copy.157
  563.7 16.6 %reshape.806 = f32[24,8,4608]{2,1,0:T(8,128)} reshape(f32[24,8,2,24,2,48]{5,4,3,2,1,0:T(2,128)} %copy.157) | data formatting | bytes 7077888 | tf_op jit(solution)/shard_map/reshape | solution.py:114
  610.8 77.6 %all-to-all-done.4 = f32[8,24,1,4608]{3,2,1,0:T(1,128)} async-done(((f32[8,24,1,4608]{3,2,1,0:T(1,128)}), f32[8,24,1,4608]{3,2,1,0:T(1,128)}, u32[]{:S(2)}, u32[]{:S(2)}) %all-to-all-start.4) | async-done | bytes 3538976 | tf_op jit(solution)/shard_map/all_to_all | solution.py:35
  688.4 11.6 reduce.4
  700.1 17.1 %reshape_reshape.7 = f32[192,2,24,2,48]{4,3,2,1,0:T(2,128)} reshape(f32[8,24,4608]{2,1,0:T(8,128)} %reduce.4) | data formatting | bytes 7077888 | tf_op jit(solution)/shard_map/reshape;reshape | solution.py:115
  717.2 25.0 %fusion.19 = f32[48,4,2,24,2,48]{0,5,3,2,1,4:T(8,128)} fusion(f32[192,2,24,2,48,1,1]{4,3,2,1,0,6,5:T(2,128)} %bitcast.264, f32[1,192,1,4,48]{1,4,0,3,2:T(8,128)S(1)} %get-tuple-element.20, f32[1,192,1,4,48]{1,4,0,3,2:T(8,128)S(1)} %get-tuple-element.19, f32[1,192,1,4,48]{1,4,0,3,2:T(8,128)S(1)} %get-tuple-element.18), kind=kOutput, calls=%fused_computation.27 | convolution fusion | flops 4077305856 | bytes 7520256 | tf_op jit(solution)/shard_map/kfzrx,rksby->xbfzsy/dot_general | solution.py:117
  742.1 13.7 %copy.159 = f32[48,4,2,24,2,48]{5,4,3,2,0,1:T(2,128)} copy(f32[48,4,2,24,2,48]{0,5,3,2,1,4:T(8,128)} %fusion.19) | data formatting | bytes 7077888 | tf_op jit(solution)/shard_map/kfzrx,rksby->xbfzsy/transpose | solution.py:117
  755.9 16.6 %reshape.807 = f32[48,4,4608]{2,0,1:T(8,128)} reshape(f32[48,4,2,24,2,48]{5,4,3,2,0,1:T(2,128)} %copy.159) | data formatting | bytes 7077888 | tf_op jit(solution)/shard_map/reshape | solution.py:118
  772.5 46.8 %all_to_all.64 = f32[48,4,4608]{2,0,1:T(8,128)} all-to-all(f32[48,4,4608]{2,0,1:T(8,128)} %reshape.807), channel_id=1, replica_groups=mesh['band'=4,'px'=4,'py'=2] {'px'}, dimensions={1} | all-to-all | bytes 7077888 | tf_op jit(solution)/shard_map/all_to_all | solution.py:30
  819.3 17.1 %reshape.808 = f32[192,2,24,2,48]{4,3,2,1,0:T(2,128)} reshape(f32[4,48,1,4608]{3,1,0,2:T(8,128)} %bitcast.270) | data formatting | bytes 7077888 | tf_op jit(solution)/shard_map/reshape | solution.py:119
  836.4 13.2 %copy.160 = f32[192,2,24,2,48]{0,4,3,2,1:T(8,128)} copy(f32[192,2,24,2,48]{4,3,2,1,0:T(2,128)} %reshape.808) | data formatting | bytes 7077888 | tf_op jit(solution)/shard_map/reshape | solution.py:119
  849.6 10.3 fusion.9
  867.3 320.4 %all-gather.2.cloned.1.call-done = f32[4,96,48,192]{3,2,1,0:T(8,128)} async-done(((f32[4,24,48,192]{3,2,1,0:T(8,128)}), f32[4,96,48,192]{3,2,1,0:T(8,128)}) %all-gather.2.cloned.1.call-update) | async-done | bytes 14155792 | tf_op jit(solution)/shard_map/all_gather | solution.py:171
  1192.6 11.8 slice.55
  (92 shorter events, 158.8 us)
Async XLA Ops:
  7.2 2.2 copy-start
  8.1 10.5 copy-start.5
  12.8 8.6 all-to-all-start
  193.1 45.9 %all-to-all-start.1 = ((bf16[4,2,221184]{2,1,0:T(2,128)(2,1)}), bf16[4,2,221184]{2,1,0:T(2,128)(2,1)}, u32[]{:S(2)}, u32[]{:S(2)}) async-start(bf16[4,2,221184]{2,1,0:T(2,128)(2,1)} %reshape.854), calls=%async_computation.1 | async-start | bytes 7077888 | tf_op jit(solution)/shard_map/all_to_all | solution.py:159
  197.8 176.6 %reduce-scatter.2.cloned.1.call-start = ((), (), s32[]{:S(2)}) async-start(), calls=%async_computation.7 | async-start | bytes 5898240 | tf_op jit(solution)/shard_map/reduce_scatter | solution.py:167
  398.0 26.1 %all-to-all-start.2 = ((f32[48,4,2304]{2,0,1:T(8,128)}), f32[48,4,2304]{2,0,1:T(8,128)S(1)}, u32[]{:S(2)}, u32[]{:S(2)}) async-start(f32[48,4,2304]{2,0,1:T(8,128)} %reshape.803), calls=%async_computation.3 | async-start | bytes 3538944 | tf_op jit(solution)/shard_map/all_to_all | solution.py:30
  464.4 46.0 %all-to-all-start.3 = ((f32[8,24,1,2304]{3,2,1,0:T(1,128)}), f32[8,24,1,2304]{3,2,1,0:T(1,128)S(1)}, u32[]{:S(2)}, u32[]{:S(2)}) async-start(f32[8,24,1,2304]{3,2,1,0:T(1,128)} %fusion.82), calls=%async_computation.4 | async-start | bytes 3538944 | tf_op jit(solution)/shard_map/all_to_all | solution.py:35
  538.0 0.9 copy-start.3
  538.1 1.0 copy-start.4
  605.4 83.1 %all-to-all-start.4 = ((f32[8,24,1,4608]{3,2,1,0:T(1,128)}), f32[8,24,1,4608]{3,2,1,0:T(1,128)}, u32[]{:S(2)}, u32[]{:S(2)}) async-start(f32[8,24,1,4608]{3,2,1,0:T(1,128)} %fusion.72), calls=%async_computation.5 | async-start | bytes 7077888 | tf_op jit(solution)/shard_map/all_to_all | solution.py:35
  609.9 577.9 %all-gather.2.cloned.1.call-start = ((), (), s32[]{:S(2)}) async-start(), calls=%async_computation.8 | async-start | bytes 23592960 | tf_op jit(solution)/shard_map/all_gather | solution.py:171
  860.3 1.3 copy-start.2
  1192.6 11.8 copy-start.1
Sparse Core Ops, SparseCore 0:
  289.2 85.1 reduce-scatter.1
  867.5 320.2 all-gather.1
